TPU v7x, 32 devices: a whole 2x2x4 slice. The times are simulated.
32 devices in a mesh: kv: 2 (over core), seq: 16 (over z, y, x), dp: 1.
Axes of the slice: x: 2, y: 2, z: 4, core: 2. Of those that a mesh axis runs over, the one named last changes fastest.
Arguments:
- token_input_state: bfloat16 [4, 8192], P('dp'), may hold values from -6 to 6
- query_matrix: bfloat16 [8192, 2048], P('seq', 'kv'), may hold values from -0.0625 to 0.0625
- key_value_weight: bfloat16 [8192, 512], P('seq', 'kv'), may hold values from -0.5 to 0.5
- output_weight: bfloat16 [2048, 8192], P('kv', 'seq'), may hold values from -0.125 to 0.125
- key_cache_rows: bfloat16 [4, 2, 32768, 128], P('dp', 'kv', 'seq'), may hold values from -6000 to 6000, as said below
- value_cache_rows: bfloat16 [4, 2, 32768, 128], P('dp', 'kv', 'seq'), may hold values from -24 to 24
- live_lengths: int32 [4, 16], P('dp'), may hold values from 2 to 2048, as said below
- owner_shard: int32 [4], P('dp'), may hold values from 0 to 15
Outputs:
- layer_out: bfloat16 [4, 8192], P('dp', 'seq')
Inputs may be any that keep to these rules, and one draw needn't show every extreme that they name: `live_lengths`: every block holds 2 to 2048 live slots; the owner's block of a sequence holds fewer than 2048; in every sequence some other block holds exactly 2048. `key_cache_rows`: bounded as stated.
All inputs are finite; a program needn't handle non-finite values.
Results may differ from a plain program's by a relative error of at most 0.015.
The roundings to bfloat16 on the way count: a program that leaves them out, or rounds other values in their place, can miss the bound.
Values may be sent and summed in bfloat16 or wider, within the bound.
A program may use at most 64 MiB of HBM per device.

v0:
```python
import math

import jax
import jax.numpy as jnp
from jax import lax
from jax.sharding import PartitionSpec as P

HEAD_SIZE = 128
QUERY_GROUP = 8


rope_theta = 500000.0


def frequencies():
    exponent = jnp.arange(0, HEAD_SIZE, 2).astype(jnp.float32) / HEAD_SIZE
    return jnp.power(rope_theta, -exponent)


def rotate(vectors, angles):
    half_size = vectors.shape[-1] // 2
    first_half = vectors[..., :half_size]
    second_half = vectors[..., half_size:]
    cosine_table = jnp.cos(angles)
    sine_table = jnp.sin(angles)
    return jnp.concatenate(
        [
            first_half * cosine_table - second_half * sine_table,
            second_half * cosine_table + first_half * sine_table,
        ],
        -1,
    )


def local(
    token_input_state,
    query_matrix,
    key_value_weight,
    output_weight,
    key_cache_rows,
    value_cache_rows,
    live_lengths,
    owner_shard,
):
    batch_rows = token_input_state.shape[0]
    kv_local = key_cache_rows.shape[1]
    slot_count = key_cache_rows.shape[2]
    row_count = query_matrix.shape[0]
    shard_index = lax.axis_index("seq")
    shard_total = lax.axis_size("seq")
    local_cols = lax.dynamic_slice_in_dim(token_input_state, shard_index * row_count, row_count, 1)
    query_part = jnp.dot(local_cols, query_matrix, preferred_element_type=jnp.float32)
    keyval_part = jnp.dot(local_cols, key_value_weight, preferred_element_type=jnp.float32)
    query_flat, keyval_flat = lax.psum((query_part, keyval_part), "seq")
    query_rows = query_flat.reshape(batch_rows, kv_local, QUERY_GROUP, HEAD_SIZE)
    key_value_rows = keyval_flat.reshape(batch_rows, kv_local, 2, HEAD_SIZE)
    columns = jnp.arange(shard_total)[None, :]
    lookup = jnp.sum(jnp.where(columns == owner_shard[:, None], live_lengths, 0), 1)
    own_length = jnp.sum(jnp.where(columns == shard_index, live_lengths, 0), 1)
    position = owner_shard * slot_count + lookup
    angles = position.astype(jnp.float32)[:, None] * frequencies()[None, :]
    query_rot = rotate(query_rows, angles[:, None, None, :]).astype(jnp.bfloat16)
    key_new = rotate(key_value_rows[:, :, 0], angles[:, None, :]).astype(jnp.bfloat16)
    value_new = key_value_rows[:, :, 1].astype(jnp.bfloat16)
    scaling = 1.0 / math.sqrt(HEAD_SIZE)
    new_score = (
        jnp.sum(query_rot.astype(jnp.float32) * key_new.astype(jnp.float32)[:, :, None, :], -1)
        * scaling
    )
    is_owner = (owner_shard == shard_index)[:, None, None]
    start_top = jnp.where(is_owner, new_score, -jnp.inf)
    scores = (
        jnp.einsum("bhgd,bhld->bhgl", query_rot, key_cache_rows, preferred_element_type=jnp.float32)
        * scaling
    )
    live_mask = jnp.arange(slot_count)[None, :] < own_length[:, None]
    scores = jnp.where(live_mask[:, None, None, :], scores, -jnp.inf)
    shard_top = jnp.maximum(jnp.max(scores, -1), start_top)
    prob_block = jnp.exp(scores - shard_top[..., None]).astype(jnp.bfloat16)
    totals = jnp.sum(prob_block, -1, dtype=jnp.float32)
    accum = jnp.einsum(
        "bhgl,bhld->bhgd", prob_block, value_cache_rows, preferred_element_type=jnp.float32
    )
    new_prob = jnp.where(is_owner, jnp.exp(new_score - shard_top), 0.0).astype(jnp.bfloat16)
    totals = totals + new_prob.astype(jnp.float32)
    accum = (
        accum
        + new_prob.astype(jnp.float32)[..., None] * value_new.astype(jnp.float32)[:, :, None, :]
    )
    overall = lax.pmax(shard_top, "seq")
    factor = jnp.exp(shard_top - overall)
    totals, accum = lax.psum((totals * factor, accum * factor[..., None]), "seq")
    attended = (
        (accum / totals[..., None])
        .astype(jnp.bfloat16)
        .reshape(batch_rows, kv_local * QUERY_GROUP * HEAD_SIZE)
    )
    partial_value = jnp.dot(attended, output_weight, preferred_element_type=jnp.float32)
    return lax.psum(partial_value, "kv").astype(jnp.bfloat16)


def solution(mesh):
    return jax.shard_map(
        local,
        mesh=mesh,
        in_specs=(
            P("dp", None),
            P("seq", "kv"),
            P("seq", "kv"),
            P("kv", "seq"),
            P("dp", "kv", "seq", None),
            P("dp", "kv", "seq", None),
            P("dp", None),
            P("dp"),
        ),
        out_specs=P("dp", "seq"),
        check_vma=False,
    )
```

profile of v0, /device:TPU:0, one launch (start us, length us, event | category | flops | bytes accessed | tf_op | source)
XLA Modules:
  0.0 201.0 jit_solution(5231457990052231082)
XLA Ops:
  0.0 0.0 copy-start
  0.0 0.8 broadcast_compare_fusion
  0.8 0.9 select_reduce_fusion
  1.7 0.7 add_convert_fusion.1
  2.4 1.1 convolution_bitcast_fusion.1
  3.5 0.1 multiply_cosine_fusion.1
  3.6 0.1 iota_compare_fusion
  3.7 1.5 convolution_bitcast_fusion
  5.2 78.6 %all-reduce.1 = (f32[4,1,8,128]{3,2,0,1:T(8,128)S(1)}, f32[4,1,2,128]{3,0,2,1:T(4,128)S(1)}) all-reduce(f32[4,1,8,128]{3,2,0,1:T(8,128)S(1)} %bitcast.75, f32[4,1,2,128]{3,0,2,1:T(4,128)S(1)} %convolution_bitcast_fusion.1), channel_id=1, replica_groups=mesh['kv'=2,'seq'=16,'dp'=1] {'seq'}, use_global_device_ids=true, to_apply=%region_1.0 | all-reduce | flops 5120 | bytes 40960 | tf_op jit(solution)/shard_map/psum | solution.py:54
  83.8 0.1 subtract_convert_fusion
  83.9 0.1 fusion.40
  84.0 0.1 maximum_convert_fusion
  84.1 0.2 multiply_reduce_fusion
  84.2 0.0 copy-done
  84.2 0.0 copy-start.1
  84.2 0.8 fusion.45
  85.0 0.1 fusion.32
  85.1 36.6 %pmax.7 = f32[4,1,8]{2,0,1:T(4,128)S(1)} all-reduce(f32[4,1,8]{2,0,1:T(4,128)S(1)} %fusion.32), channel_id=1, replica_groups=mesh['kv'=2,'seq'=16,'dp'=1] {'seq'}, use_global_device_ids=true, to_apply=%region_6.7 | all-reduce | flops 32 | bytes 256 | tf_op jit(solution)/shard_map/pmax | solution.py:90
  121.6 0.1 fusion.36
  121.7 0.2 convert_reduce_fusion
  121.9 0.1 fusion.31
  122.0 2.0 %fusion.10 = f32[4,1,8,128]{3,2,0,1:T(8,128)S(1)} fusion(bf16[4,1,2048,128]{3,2,1,0:T(8,128)(2,1)} %param.13, f32[4,8,2048]{2,1,0:T(8,128)S(1)} %get-tuple-element.22, f32[4,8]{1,0:T(4,128)S(1)} %get-tuple-element.14, f32[4,8]{1,0:T(4,128)S(1)} %get-tuple-element.16, f32[4,128]{1,0:T(4,128)S(1)} %fusion.38, f32[4,8]{1,0:T(4,128)S(1)} %get-tuple-element.13), kind=kOutput, calls=%fused_computation.7 | convolution fusion | flops 16920576 | bytes 2378112 | tf_op jit(solution)/shard_map/bhgl,bhld->bhgd/dot_general | solution.py:81
  124.0 73.6 %all-reduce = (f32[4,1,8,128]{3,2,0,1:T(8,128)S(1)}, f32[4,8]{1,0:T(4,128)S(1)}) all-reduce(f32[4,1,8,128]{3,2,0,1:T(8,128)S(1)} %fusion.10, f32[4,8]{1,0:T(4,128)S(1)} %get-tuple-element.15), channel_id=1, replica_groups=mesh['kv'=2,'seq'=16,'dp'=1] {'seq'}, use_global_device_ids=true, to_apply=%region_7.8 | all-reduce | flops 4128 | bytes 33024 | tf_op jit(solution)/shard_map/psum | solution.py:92
  197.6 0.1 fusion.19
  197.7 0.0 copy-done.1
  197.7 0.2 fusion.13
  198.0 3.1 %psum.39 = bf16[4,512]{1,0:T(4,128)(2,1)} all-reduce(f32[4,512]{1,0:T(4,128)S(1)} %fusion.13), channel_id=1, replica_groups=mesh['kv'=2,'seq'=16,'dp'=1] {'kv'}, use_global_device_ids=true, to_apply=%region_10.11 | all-reduce | flops 2048 | bytes 12288 | tf_op jit(solution)/shard_map/psum | solution.py:99
  (5 shorter events, 0.0 us)
Async XLA Ops:
  0.0 84.2 %copy-start = (bf16[4,1,2048,128]{3,2,1,0:T(8,128)(2,1)S(1)}, bf16[4,1,2048,128]{3,2,1,0:T(8,128)(2,1)}, u32[]{:S(2)}) copy-start(bf16[4,1,2048,128]{3,2,1,0:T(8,128)(2,1)} %param.12) | copy-start | bytes 6291460
  84.2 113.5 %copy-start.1 = (bf16[1024,512]{1,0:T(8,128)(2,1)S(1)}, bf16[1024,512]{1,0:T(8,128)(2,1)}, u32[]{:S(2)}) copy-start(bf16[1024,512]{1,0:T(8,128)(2,1)} %param.11) | copy-start | bytes 3145732
where the time goes:
time: 201 us
  blocking collectives  192 us (96%)
  matrix products  5.64 us (3%)
  other arithmetic  3.5 us (2%)
    psum x1, blocking collectives, local(): query_flat, keyval_flat = lax.psum((query_part, keyval_part), 'seq')  78.6 us
    psum x1, blocking collectives, local(): lax.psum((totals * factor, accum * factor[..., None]), 'seq')  73.6 us
    pmax x1, blocking collectives, local(): overall = lax.pmax(shard_top, 'seq')  36.6 us

commit v1 on v0

v1 whole, which is shorter than its diff:
```python
import functools
import math

import jax
import jax.numpy as jnp
import numpy as np
from jax import lax
from jax.experimental import pallas as pl
from jax.experimental.pallas import tpu as pltpu
from jax.sharding import PartitionSpec as P

ROPE_THETA = 500000.0
F32 = jnp.float32
BF16 = jnp.bfloat16


def gather_start(buf, rank, count, send_sem, recv_sem, peer_of):
    copies = []
    for d in range(1, count):
        j = lax.rem(rank + d, count)
        cp = pltpu.make_async_remote_copy(
            src_ref=buf.at[rank],
            dst_ref=buf.at[rank],
            send_sem=send_sem.at[d],
            recv_sem=recv_sem.at[rank],
            device_id=peer_of(j),
            device_id_type=pl.DeviceIdType.MESH,
        )
        cp.start()
        copies.append(cp)
    return copies


def gather_wait(buf, rank, count, send_sem, recv_sem, peer_of):
    for d in range(1, count):
        j = lax.rem(rank + d, count)
        pltpu.make_async_remote_copy(
            src_ref=buf.at[j],
            dst_ref=buf.at[j],
            send_sem=send_sem.at[d],
            recv_sem=recv_sem.at[j],
            device_id=peer_of(j),
            device_id_type=pl.DeviceIdType.MESH,
        ).wait_recv()


def kernel(
    inner, outer, kv_size, group, head,
    live, owner, freq, x_hbm, wq_hbm, wkv_hbm, wo_hbm, k_hbm, v_hbm,
    out,
    x, wq, wkv, wo, keys, vals,
    part_in, part_out, acc_in, acc_out, kv_buf, q_rows, att_rows,
    load_sem, sa, ra, sb, rb, sc, rc, sd, rd, se, re,
):
    me = lax.axis_index("seq")
    kv = lax.axis_index("kv")
    batch = x.shape[0]
    rows = wq.shape[0]
    qw = wq.shape[1]
    slots = keys.shape[2]
    plane = me // inner
    spot = lax.rem(me, inner)

    def inner_peer(j):
        return {"seq": plane * inner + j}

    def outer_peer(j):
        return {"seq": j * inner + spot}

    def kv_peer(j):
        return {"kv": j}

    barrier = pltpu.get_barrier_semaphore()
    for d in range(1, inner):
        pl.semaphore_signal(barrier, inc=1, device_id=inner_peer(lax.rem(spot + d, inner)),
                            device_id_type=pl.DeviceIdType.MESH)
    for d in range(1, outer):
        pl.semaphore_signal(barrier, inc=1, device_id=outer_peer(lax.rem(plane + d, outer)),
                            device_id_type=pl.DeviceIdType.MESH)
    for d in range(1, kv_size):
        pl.semaphore_signal(barrier, inc=1, device_id=kv_peer(lax.rem(kv + d, kv_size)),
                            device_id_type=pl.DeviceIdType.MESH)

    first = pl.multiple_of(me * rows, rows)
    loads = [
        pltpu.make_async_copy(x_hbm.at[:, pl.ds(first, rows)], x, load_sem.at[0]),
        pltpu.make_async_copy(wq_hbm, wq, load_sem.at[1]),
        pltpu.make_async_copy(wkv_hbm, wkv, load_sem.at[2]),
        pltpu.make_async_copy(k_hbm, keys, load_sem.at[3]),
        pltpu.make_async_copy(v_hbm, vals, load_sem.at[4]),
        pltpu.make_async_copy(wo_hbm, wo, load_sem.at[5]),
    ]
    for cp in loads:
        cp.start()

    row_id = lax.broadcasted_iota(jnp.int32, (batch, head), 0)
    lane_id = lax.broadcasted_iota(jnp.int32, (batch, head), 1)
    position = jnp.zeros((batch, head), jnp.int32)
    for b in range(batch):
        own = owner[b]
        position = jnp.where(row_id == b, own * slots + live[b, own], position)
    angle = position.astype(F32) * freq[...]
    cosine = jnp.cos(angle)
    sine = jnp.sin(angle)
    sine = jnp.where(lane_id < head // 2, -sine, sine)

    def rotate(v):
        return v * cosine + pltpu.roll(v, head // 2, 1) * sine

    for cp in loads[:3]:
        cp.wait()
    xs = x[...]
    part_in[spot, :, :qw] = jnp.dot(xs, wq[...], preferred_element_type=F32)
    part_in[spot, :, qw:] = jnp.dot(xs, wkv[...], preferred_element_type=F32)
    pl.semaphore_wait(barrier, inner + outer + kv_size - 3)

    sends = gather_start(part_in, spot, inner, sa, ra, inner_peer)
    gather_wait(part_in, spot, inner, sa, ra, inner_peer)
    total = part_in[0]
    for j in range(1, inner):
        total = total + part_in[j]
    part_out[plane] = total
    sends += gather_start(part_out, plane, outer, sb, rb, outer_peer)
    gather_wait(part_out, plane, outer, sb, rb, outer_peer)
    total = part_out[0]
    for j in range(1, outer):
        total = total + part_out[j]

    for h in range(group):
        q_rows[:, h, :] = rotate(total[:, h * head:(h + 1) * head])
    key_new = rotate(total[:, qw:qw + head]).astype(BF16).astype(F32)
    value_new = total[:, qw + head:qw + 2 * head].astype(BF16).astype(F32)

    loads[3].wait()
    loads[4].wait()
    scaling = 1.0 / math.sqrt(head)
    slot_id = lax.broadcasted_iota(jnp.int32, (group, slots), 1)
    stat_lane = lax.broadcasted_iota(jnp.int32, (group, head), 1)
    stat = jnp.zeros((group, head), F32)
    for b in range(batch):
        q = q_rows[b].astype(BF16)
        new_score = jnp.sum(q.astype(F32) * key_new[b:b + 1], -1, keepdims=True) * scaling
        new_score = jnp.where(owner[b] == me, new_score, -jnp.inf)
        s = lax.dot_general(q, keys[b, 0], (((1,), (1,)), ((), ())), preferred_element_type=F32)
        s = jnp.where(slot_id < live[b, me], s * scaling, -jnp.inf)
        top = jnp.maximum(jnp.max(s, -1, keepdims=True), new_score)
        prob = jnp.exp(s - top).astype(BF16)
        new_prob = jnp.exp(new_score - top).astype(BF16).astype(F32)
        count = jnp.sum(prob.astype(F32), -1, keepdims=True) + new_prob
        acc = jnp.dot(prob, vals[b, 0], preferred_element_type=F32)
        acc_in[spot, b * group:(b + 1) * group] = acc + new_prob * value_new[b:b + 1]
        stat = jnp.where(stat_lane == b, top, stat)
        stat = jnp.where(stat_lane == batch + b, count, stat)
    acc_in[spot, batch * group:] = stat

    def merge(buf, members):
        stats = [buf[j, batch * group:] for j in range(members)]
        top = stats[0]
        for t in stats[1:]:
            top = jnp.maximum(top, t)
        factors = [jnp.exp(jnp.where(stat_lane < batch, t - top, 0.0)) for t in stats]
        count = None
        for f, t in zip(factors, stats):
            term = f * pltpu.roll(t, head - batch, 1)
            count = term if count is None else count + term
        sums = []
        for b in range(batch):
            acc = None
            for j in range(members):
                term = factors[j][:, b:b + 1] * buf[j, b * group:(b + 1) * group]
                acc = term if acc is None else acc + term
            sums.append(acc)
        return top, count, sums

    sends += gather_start(acc_in, spot, inner, sc, rc, inner_peer)
    gather_wait(acc_in, spot, inner, sc, rc, inner_peer)
    top, count, sums = merge(acc_in, inner)
    for b in range(batch):
        acc_out[plane, b * group:(b + 1) * group] = sums[b]
    acc_out[plane, batch * group:] = jnp.where(stat_lane < batch, top, pltpu.roll(count, batch, 1))
    sends += gather_start(acc_out, plane, outer, sd, rd, outer_peer)
    gather_wait(acc_out, plane, outer, sd, rd, outer_peer)
    top, count, sums = merge(acc_out, outer)
    for b in range(batch):
        att_rows[b] = sums[b] / count[:, b:b + 1]
    attended = jnp.concatenate([att_rows[:, h, :].astype(BF16) for h in range(group)], -1)

    loads[5].wait()
    kv_buf[kv] = jnp.dot(attended, wo[...], preferred_element_type=F32)
    sends += gather_start(kv_buf, kv, kv_size, se, re, kv_peer)
    gather_wait(kv_buf, kv, kv_size, se, re, kv_peer)
    total = kv_buf[0]
    for j in range(1, kv_size):
        total = total + kv_buf[j]
    out[...] = total.astype(BF16)
    for cp in sends:
        cp.wait_send()


def local(n, kv_size, x, wq, wkv, wo, keys, vals, live, owner):
    batch = x.shape[0]
    head = keys.shape[3]
    rows, qw = wq.shape
    group = qw // head
    cols = wo.shape[1]
    inner = 1
    while inner * inner < n and n % (inner * 2) == 0:
        inner *= 2
    outer = n // inner
    half = np.float64(ROPE_THETA) ** (-np.arange(0, head, 2, dtype=np.float64) / head)
    freq = jnp.asarray(np.concatenate([half, half]).astype(np.float32)[None, :])
    dma = pltpu.SemaphoreType.DMA
    acc_rows = batch * group + group
    smem = pl.BlockSpec(memory_space=pltpu.SMEM)
    vmem = pl.BlockSpec(memory_space=pltpu.VMEM)
    hbm = pl.BlockSpec(memory_space=pl.ANY)
    return pl.pallas_call(
        functools.partial(kernel, inner, outer, kv_size, group, head),
        out_shape=jax.ShapeDtypeStruct((batch, cols), BF16),
        in_specs=[smem, smem, vmem] + [hbm] * 6,
        out_specs=vmem,
        scratch_shapes=[
            pltpu.VMEM((batch, rows), BF16),
            pltpu.VMEM(wq.shape, BF16),
            pltpu.VMEM(wkv.shape, BF16),
            pltpu.VMEM(wo.shape, BF16),
            pltpu.VMEM(keys.shape, BF16),
            pltpu.VMEM(vals.shape, BF16),
            pltpu.VMEM((inner, batch, qw + wkv.shape[1]), F32),
            pltpu.VMEM((outer, batch, qw + wkv.shape[1]), F32),
            pltpu.VMEM((inner, acc_rows, head), F32),
            pltpu.VMEM((outer, acc_rows, head), F32),
            pltpu.VMEM((kv_size, batch, cols), F32),
            pltpu.VMEM((batch, group, head), F32),
            pltpu.VMEM((batch, group, head), F32),
            dma((6,)),
            dma((inner,)), dma((inner,)),
            dma((outer,)), dma((outer,)),
            dma((inner,)), dma((inner,)),
            dma((outer,)), dma((outer,)),
            dma((kv_size,)), dma((kv_size,)),
        ],
        compiler_params=pltpu.CompilerParams(collective_id=0, has_side_effects=True),
    )(live, owner, freq, x, wq, wkv, wo, keys, vals)


def solution(mesh):
    return jax.shard_map(
        functools.partial(local, mesh.shape["seq"], mesh.shape["kv"]),
        mesh=mesh,
        in_specs=(
            P("dp", None),
            P("seq", "kv"),
            P("seq", "kv"),
            P("kv", "seq"),
            P("dp", "kv", "seq", None),
            P("dp", "kv", "seq", None),
            P("dp", None),
            P("dp"),
        ),
        out_specs=P("dp", "seq"),
        check_vma=False,
    )
```

time: 201 us -> 26.3 us (0.13)
  blocking collectives: 192 us -> 0 us
  Pallas kernels: 0 us -> 24.8 us
  matrix products: 5.64 us -> 0 us
  other arithmetic: 3.5 us -> 0 us
    psum x3 -> x0, blocking collectives: 155 us -> none  [the longest x1 78.6 us: local(): query_flat, keyval_flat = lax.psum((query_part, keyval_part), 'seq')]
    pmax x1 -> x0, blocking collectives: 36.6 us -> none  [local(): overall = lax.pmax(shard_top, 'seq')]
    pallas_call x0 -> x1, Pallas kernels: none -> 24.8 us  [local(): pl.pallas_call(functools.partial(kernel, inner, outer, kv_size, group, he...]
    dot_general x5 -> x0, matrix products: 5.64 us -> none  [the longest x1 2.03 us: local(): jnp.einsum('bhgl,bhld->bhgd', prob_block, value_cache_rows, preferred_ele...]
where the time goes in v1:
time: 26.3 us; the launch traced here: 26 us
  Pallas kernels  24.8 us (94%)
  local copies, waits for them, and re-layouts  1.28 us (5%)
    pallas_call x1, Pallas kernels, local(): pl.pallas_call(functools.partial(kernel, inner, outer, kv_size, group, he...  24.8 us
    unnamed x1, local copies, waits for them, and re-layouts  1.28 us

profile of v1, /device:TPU:0, one launch (start us, length us, event | category | flops | bytes accessed | tf_op | source)
XLA Modules:
  0.0 26.0 jit_solution(1401429591048087877)
XLA Ops:
  0.0 24.8 %shard_map.91 = bf16[4,512]{1,0:T(4,128)(2,1)} custom-call(s32[4,16]{1,0:T(4,128)} %live.1, s32[4]{0:T(128)} %owner.1, f32[1,128]{1,0:T(1,128)} %constant.2.clone.freq, bf16[4,8192]{1,0:T(4,128)(2,1)} %x_hbm.1, bf16[512,1024]{1,0:T(8,128)(2,1)} %wq_hbm.1, bf16[512,256]{1,0:T(8,128)(2,1)} %wkv_hbm.1, bf16[1024,512]{1,0:T(8,128)(2,1)} %wo_hbm.1, ...), custom_call_target="tpu_custom_call" | custom-call | tf_op jit(solution)/shard_map/pallas_call | solution.py:217
  24.8 1.3 %copy.11 = bf16[4,512]{1,0:T(4,128)(2,1)} copy(bf16[4,512]{1,0:T(4,128)(2,1)} %shard_map.91) | data formatting | bytes 8192

commit v2 on v1

--- a/solution.py
+++ b/solution.py
@@ -49,8 +49,8 @@
     live, owner, freq, x_hbm, wq_hbm, wkv_hbm, wo_hbm, k_hbm, v_hbm,
     out,
     x, wq, wkv, wo, keys, vals,
-    part_in, part_out, acc_in, acc_out, kv_buf, q_rows, att_rows,
-    load_sem, sa, ra, sb, rb, sc, rc, sd, rd, se, re,
+    qa_in, qa_out, qb_in, qb_out, aa_in, aa_out, ab_in, ab_out, kv_buf, q_rows, att_rows,
+    load_sem, inner_sem, outer_sem, kv_sem,
 ):
     me = lax.axis_index("seq")
     kv = lax.axis_index("kv")
@@ -90,8 +90,28 @@
         pltpu.make_async_copy(v_hbm, vals, load_sem.at[4]),
         pltpu.make_async_copy(wo_hbm, wo, load_sem.at[5]),
     ]
-    for cp in loads:
+    for cp in loads[:3]:
         cp.start()
+
+    sends = []
+
+    def inner_start(buf, i):
+        sends.extend(gather_start(buf, spot, inner, inner_sem.at[2 * i], inner_sem.at[2 * i + 1], inner_peer))
+
+    def inner_wait(buf, i):
+        gather_wait(buf, spot, inner, inner_sem.at[2 * i], inner_sem.at[2 * i + 1], inner_peer)
+
+    def outer_start(buf, i):
+        sends.extend(gather_start(buf, plane, outer, outer_sem.at[2 * i], outer_sem.at[2 * i + 1], outer_peer))
+
+    def outer_wait(buf, i):
+        gather_wait(buf, plane, outer, outer_sem.at[2 * i], outer_sem.at[2 * i + 1], outer_peer)
+
+    def add_up(buf, members):
+        total = buf[0]
+        for j in range(1, members):
+            total = total + buf[j]
+        return total
 
     row_id = lax.broadcasted_iota(jnp.int32, (batch, head), 0)
     lane_id = lax.broadcasted_iota(jnp.int32, (batch, head), 1)
@@ -109,22 +129,26 @@
 
     for cp in loads[:3]:
         cp.wait()
+    for cp in loads[3:]:
+        cp.start()
     xs = x[...]
-    part_in[spot, :, :qw] = jnp.dot(xs, wq[...], preferred_element_type=F32)
-    part_in[spot, :, qw:] = jnp.dot(xs, wkv[...], preferred_element_type=F32)
+    cut = qa_in.shape[2]
+    qa_in[spot] = jnp.dot(xs, wq[:, :cut], preferred_element_type=F32)
+    qb_out[plane, :, :qw - cut] = jnp.dot(xs, wq[:, cut:], preferred_element_type=F32)
+    qb_out[plane, :, qw - cut:] = jnp.dot(xs, wkv[...], preferred_element_type=F32)
     pl.semaphore_wait(barrier, inner + outer + kv_size - 3)
 
-    sends = gather_start(part_in, spot, inner, sa, ra, inner_peer)
-    gather_wait(part_in, spot, inner, sa, ra, inner_peer)
-    total = part_in[0]
-    for j in range(1, inner):
-        total = total + part_in[j]
-    part_out[plane] = total
-    sends += gather_start(part_out, plane, outer, sb, rb, outer_peer)
-    gather_wait(part_out, plane, outer, sb, rb, outer_peer)
-    total = part_out[0]
-    for j in range(1, outer):
-        total = total + part_out[j]
+    inner_start(qa_in, 0)
+    outer_start(qb_out, 0)
+    inner_wait(qa_in, 0)
+    qa_out[plane] = add_up(qa_in, inner)
+    outer_start(qa_out, 1)
+    outer_wait(qb_out, 0)
+    qb_in[spot] = add_up(qb_out, outer)
+    inner_start(qb_in, 1)
+    outer_wait(qa_out, 1)
+    inner_wait(qb_in, 1)
+    total = jnp.concatenate([add_up(qa_out, outer), add_up(qb_in, inner)], -1)
 
     for h in range(group):
         q_rows[:, h, :] = rotate(total[:, h * head:(h + 1) * head])
@@ -136,8 +160,8 @@
     scaling = 1.0 / math.sqrt(head)
     slot_id = lax.broadcasted_iota(jnp.int32, (group, slots), 1)
     stat_lane = lax.broadcasted_iota(jnp.int32, (group, head), 1)
-    stat = jnp.zeros((group, head), F32)
-    for b in range(batch):
+
+    def attend(b):
         q = q_rows[b].astype(BF16)
         new_score = jnp.sum(q.astype(F32) * key_new[b:b + 1], -1, keepdims=True) * scaling
         new_score = jnp.where(owner[b] == me, new_score, -jnp.inf)
@@ -148,23 +172,31 @@
         new_prob = jnp.exp(new_score - top).astype(BF16).astype(F32)
         count = jnp.sum(prob.astype(F32), -1, keepdims=True) + new_prob
         acc = jnp.dot(prob, vals[b, 0], preferred_element_type=F32)
-        acc_in[spot, b * group:(b + 1) * group] = acc + new_prob * value_new[b:b + 1]
-        stat = jnp.where(stat_lane == b, top, stat)
-        stat = jnp.where(stat_lane == batch + b, count, stat)
-    acc_in[spot, batch * group:] = stat
+        return top, count, acc + new_prob * value_new[b:b + 1]
+
+    def attend_half(buf, slot, ids):
+        nb = len(ids)
+        stat = jnp.zeros((group, head), F32)
+        for i, b in enumerate(ids):
+            top, count, acc = attend(b)
+            buf[slot, i * group:(i + 1) * group] = acc
+            stat = jnp.where(stat_lane == i, top, stat)
+            stat = jnp.where(stat_lane == nb + i, count, stat)
+        buf[slot, nb * group:] = stat
 
     def merge(buf, members):
-        stats = [buf[j, batch * group:] for j in range(members)]
+        nb = buf.shape[1] // group - 1
+        stats = [buf[j, nb * group:] for j in range(members)]
         top = stats[0]
         for t in stats[1:]:
             top = jnp.maximum(top, t)
-        factors = [jnp.exp(jnp.where(stat_lane < batch, t - top, 0.0)) for t in stats]
+        factors = [jnp.exp(jnp.where(stat_lane < nb, t - top, 0.0)) for t in stats]
         count = None
         for f, t in zip(factors, stats):
-            term = f * pltpu.roll(t, head - batch, 1)
+            term = f * pltpu.roll(t, head - nb, 1)
             count = term if count is None else count + term
         sums = []
-        for b in range(batch):
+        for b in range(nb):
             acc = None
             for j in range(members):
                 term = factors[j][:, b:b + 1] * buf[j, b * group:(b + 1) * group]
@@ -172,27 +204,41 @@
             sums.append(acc)
         return top, count, sums
 
-    sends += gather_start(acc_in, spot, inner, sc, rc, inner_peer)
-    gather_wait(acc_in, spot, inner, sc, rc, inner_peer)
-    top, count, sums = merge(acc_in, inner)
-    for b in range(batch):
-        acc_out[plane, b * group:(b + 1) * group] = sums[b]
-    acc_out[plane, batch * group:] = jnp.where(stat_lane < batch, top, pltpu.roll(count, batch, 1))
-    sends += gather_start(acc_out, plane, outer, sd, rd, outer_peer)
-    gather_wait(acc_out, plane, outer, sd, rd, outer_peer)
-    top, count, sums = merge(acc_out, outer)
-    for b in range(batch):
-        att_rows[b] = sums[b] / count[:, b:b + 1]
+    def merge_into(buf, members, dst, slot):
+        nb = buf.shape[1] // group - 1
+        top, count, sums = merge(buf, members)
+        for b in range(nb):
+            dst[slot, b * group:(b + 1) * group] = sums[b]
+        dst[slot, nb * group:] = jnp.where(stat_lane < nb, top, pltpu.roll(count, nb, 1))
+
+    def finish(buf, members, ids):
+        top, count, sums = merge(buf, members)
+        for i, b in enumerate(ids):
+            att_rows[b] = sums[i] / count[:, i:i + 1]
+
+    ids_a = list(range(batch // 2))
+    ids_b = list(range(batch // 2, batch))
+    attend_half(ab_out, plane, ids_b)
+    outer_start(ab_out, 2)
+    attend_half(aa_in, spot, ids_a)
+    inner_start(aa_in, 2)
+    inner_wait(aa_in, 2)
+    merge_into(aa_in, inner, aa_out, plane)
+    outer_start(aa_out, 3)
+    outer_wait(ab_out, 2)
+    merge_into(ab_out, outer, ab_in, spot)
+    inner_start(ab_in, 3)
+    inner_wait(ab_in, 3)
+    finish(ab_in, inner, ids_b)
+    outer_wait(aa_out, 3)
+    finish(aa_out, outer, ids_a)
     attended = jnp.concatenate([att_rows[:, h, :].astype(BF16) for h in range(group)], -1)
 
     loads[5].wait()
     kv_buf[kv] = jnp.dot(attended, wo[...], preferred_element_type=F32)
-    sends += gather_start(kv_buf, kv, kv_size, se, re, kv_peer)
-    gather_wait(kv_buf, kv, kv_size, se, re, kv_peer)
-    total = kv_buf[0]
-    for j in range(1, kv_size):
-        total = total + kv_buf[j]
-    out[...] = total.astype(BF16)
+    sends.extend(gather_start(kv_buf, kv, kv_size, kv_sem.at[0], kv_sem.at[1], kv_peer))
+    gather_wait(kv_buf, kv, kv_size, kv_sem.at[0], kv_sem.at[1], kv_peer)
+    out[...] = add_up(kv_buf, kv_size)
     for cp in sends:
         cp.wait_send()
 
@@ -210,13 +256,16 @@
     half = np.float64(ROPE_THETA) ** (-np.arange(0, head, 2, dtype=np.float64) / head)
     freq = jnp.asarray(np.concatenate([half, half]).astype(np.float32)[None, :])
     dma = pltpu.SemaphoreType.DMA
-    acc_rows = batch * group + group
+    width = qw + wkv.shape[1]
+    cut = width // (2 * head) * head
+    rows_a = (batch // 2 + 1) * group
+    rows_b = (batch - batch // 2 + 1) * group
     smem = pl.BlockSpec(memory_space=pltpu.SMEM)
     vmem = pl.BlockSpec(memory_space=pltpu.VMEM)
     hbm = pl.BlockSpec(memory_space=pl.ANY)
     return pl.pallas_call(
         functools.partial(kernel, inner, outer, kv_size, group, head),
-        out_shape=jax.ShapeDtypeStruct((batch, cols), BF16),
+        out_shape=pltpu.VMEM((batch, cols), F32),
         in_specs=[smem, smem, vmem] + [hbm] * 6,
         out_specs=vmem,
         scratch_shapes=[
@@ -226,22 +275,24 @@
             pltpu.VMEM(wo.shape, BF16),
             pltpu.VMEM(keys.shape, BF16),
             pltpu.VMEM(vals.shape, BF16),
-            pltpu.VMEM((inner, batch, qw + wkv.shape[1]), F32),
-            pltpu.VMEM((outer, batch, qw + wkv.shape[1]), F32),
-            pltpu.VMEM((inner, acc_rows, head), F32),
-            pltpu.VMEM((outer, acc_rows, head), F32),
+            pltpu.VMEM((inner, batch, cut), F32),
+            pltpu.VMEM((outer, batch, cut), F32),
+            pltpu.VMEM((inner, batch, width - cut), F32),
+            pltpu.VMEM((outer, batch, width - cut), F32),
+            pltpu.VMEM((inner, rows_a, head), F32),
+            pltpu.VMEM((outer, rows_a, head), F32),
+            pltpu.VMEM((inner, rows_b, head), F32),
+            pltpu.VMEM((outer, rows_b, head), F32),
             pltpu.VMEM((kv_size, batch, cols), F32),
             pltpu.VMEM((batch, group, head), F32),
             pltpu.VMEM((batch, group, head), F32),
             dma((6,)),
-            dma((inner,)), dma((inner,)),
-            dma((outer,)), dma((outer,)),
-            dma((inner,)), dma((inner,)),
-            dma((outer,)), dma((outer,)),
-            dma((kv_size,)), dma((kv_size,)),
+            dma((8, inner)),
+            dma((8, outer)),
+            dma((2, kv_size)),
         ],
         compiler_params=pltpu.CompilerParams(collective_id=0, has_side_effects=True),
-    )(live, owner, freq, x, wq, wkv, wo, keys, vals)
+    )(live, owner, freq, x, wq, wkv, wo, keys, vals).astype(BF16)
 
 
 def solution(mesh):

time: 26.3 us -> 24.8 us (0.943)
  local copies, waits for them, and re-layouts: 1.28 us -> 0 us
  Pallas kernels: 24.8 us -> 24 us
  other arithmetic: 0 us -> 0.6 us
    unnamed x1 -> x0, local copies, waits for them, and re-layouts: 1.28 us -> none
    pallas_call x1, Pallas kernels: 24.8 us -> 24 us  [local(): pl.pallas_call(functools.partial(kernel, inner, outer, kv_size, group, he...]
    convert_element_type x0 -> x1, other arithmetic: none -> 0.6 us  [local(): return pl.pallas_call(functools.partial(kernel, inner, outer, kv_size, gr...]
where the time goes in v2:
time: 24.8 us; the launch traced here: 24.6 us
  Pallas kernels  24 us (97%)
  other arithmetic  0.6 us (2%)
    pallas_call x1, Pallas kernels, local(): pl.pallas_call(functools.partial(kernel, inner, outer, kv_size, group, he...  24 us
    convert_element_type x1, other arithmetic, local(): return pl.pallas_call(functools.partial(kernel, inner, outer, kv_size, gr...  0.6 us

profile of v2, /device:TPU:0, one launch (start us, length us, event | category | flops | bytes accessed | tf_op | source)
XLA Modules:
  0.0 24.6 jit_solution(1127838552041566750)
XLA Ops:
  0.0 24.0 %shard_map.91 = f32[4,512]{1,0:T(4,128)S(1)} custom-call(s32[4,16]{1,0:T(4,128)} %live.1, s32[4]{0:T(128)} %owner.1, f32[1,128]{1,0:T(1,128)} %constant.2.clone.freq, bf16[4,8192]{1,0:T(4,128)(2,1)} %x_hbm.1, bf16[512,1024]{1,0:T(8,128)(2,1)} %wq_hbm.1, bf16[512,256]{1,0:T(8,128)(2,1)} %wkv_hbm.1, bf16[1024,512]{1,0:T(8,128)(2,1)} %wo_hbm.1, ...), custom_call_target="tpu_custom_call" | custom-call | tf_op jit(solution)/shard_map/pallas_call | solution.py:266
  24.0 0.6 %convert_element_type.3 = bf16[4,512]{1,0:T(4,128)(2,1)} convert(f32[4,512]{1,0:T(4,128)S(1)} %shard_map.91) | non-fusion elementwise | flops 2048 | bytes 12288 | tf_op jit(solution)/shard_map/convert_element_type | solution.py:295

commit v3 on v1

--- a/solution.py
+++ b/solution.py
@@ -45,11 +45,11 @@
 
 
 def kernel(
-    inner, outer, kv_size, group, head,
+    n, inner, outer, kv_size, group, head,
     live, owner, freq, x_hbm, wq_hbm, wkv_hbm, wo_hbm, k_hbm, v_hbm,
     out,
     x, wq, wkv, wo, keys, vals,
-    part_in, part_out, acc_in, acc_out, kv_buf, q_rows, att_rows,
+    part_in, part_out, acc_all, stat_all, kv_buf, q_rows, att_rows,
     load_sem, sa, ra, sb, rb, sc, rc, sd, rd, se, re,
 ):
     me = lax.axis_index("seq")
@@ -67,6 +67,9 @@
     def outer_peer(j):
         return {"seq": j * inner + spot}
 
+    def seq_peer(j):
+        return {"seq": j}
+
     def kv_peer(j):
         return {"kv": j}
 
@@ -90,7 +93,7 @@
         pltpu.make_async_copy(v_hbm, vals, load_sem.at[4]),
         pltpu.make_async_copy(wo_hbm, wo, load_sem.at[5]),
     ]
-    for cp in loads:
+    for cp in loads[:3]:
         cp.start()
 
     row_id = lax.broadcasted_iota(jnp.int32, (batch, head), 0)
@@ -109,6 +112,8 @@
 
     for cp in loads[:3]:
         cp.wait()
+    for cp in loads[3:]:
+        cp.start()
     xs = x[...]
     part_in[spot, :, :qw] = jnp.dot(xs, wq[...], preferred_element_type=F32)
     part_in[spot, :, qw:] = jnp.dot(xs, wkv[...], preferred_element_type=F32)
@@ -136,7 +141,10 @@
     scaling = 1.0 / math.sqrt(head)
     slot_id = lax.broadcasted_iota(jnp.int32, (group, slots), 1)
     stat_lane = lax.broadcasted_iota(jnp.int32, (group, head), 1)
+    stat_row = lax.broadcasted_iota(jnp.int32, (group, head), 0)
+    pairs = batch * group
     stat = jnp.zeros((group, head), F32)
+    accs = []
     for b in range(batch):
         q = q_rows[b].astype(BF16)
         new_score = jnp.sum(q.astype(F32) * key_new[b:b + 1], -1, keepdims=True) * scaling
@@ -148,41 +156,26 @@
         new_prob = jnp.exp(new_score - top).astype(BF16).astype(F32)
         count = jnp.sum(prob.astype(F32), -1, keepdims=True) + new_prob
         acc = jnp.dot(prob, vals[b, 0], preferred_element_type=F32)
-        acc_in[spot, b * group:(b + 1) * group] = acc + new_prob * value_new[b:b + 1]
-        stat = jnp.where(stat_lane == b, top, stat)
-        stat = jnp.where(stat_lane == batch + b, count, stat)
-    acc_in[spot, batch * group:] = stat
-
-    def merge(buf, members):
-        stats = [buf[j, batch * group:] for j in range(members)]
-        top = stats[0]
-        for t in stats[1:]:
-            top = jnp.maximum(top, t)
-        factors = [jnp.exp(jnp.where(stat_lane < batch, t - top, 0.0)) for t in stats]
-        count = None
-        for f, t in zip(factors, stats):
-            term = f * pltpu.roll(t, head - batch, 1)
-            count = term if count is None else count + term
-        sums = []
-        for b in range(batch):
-            acc = None
-            for j in range(members):
-                term = factors[j][:, b:b + 1] * buf[j, b * group:(b + 1) * group]
-                acc = term if acc is None else acc + term
-            sums.append(acc)
-        return top, count, sums
-
-    sends += gather_start(acc_in, spot, inner, sc, rc, inner_peer)
-    gather_wait(acc_in, spot, inner, sc, rc, inner_peer)
-    top, count, sums = merge(acc_in, inner)
+        accs.append(acc + new_prob * value_new[b:b + 1])
+        stat = jnp.where(stat_lane == b * group + stat_row, top, stat)
+        stat = jnp.where(stat_lane == pairs + b * group + stat_row, count, stat)
+    stat_all[me] = jnp.sum(stat, 0, keepdims=True)
+    acc_all[me] = jnp.concatenate(accs, 0).astype(BF16)
+
+    sends += gather_start(stat_all, me, n, sd, rd, seq_peer)
+    sends += gather_start(acc_all, me, n, sc, rc, seq_peer)
+    gather_wait(stat_all, me, n, sd, rd, seq_peer)
+    stats = stat_all[:, 0, :]
+    factor = jnp.exp(stats - jnp.max(stats, 0, keepdims=True))
+    whole = jnp.sum(factor * pltpu.roll(stats, head - pairs, 1), 0, keepdims=True)
+    lane = lax.broadcasted_iota(jnp.int32, stats.shape, 1)
+    weight = jnp.where(lane < pairs, factor / whole, 0.0).T
+    gather_wait(acc_all, me, n, sc, rc, seq_peer)
+    total = weight[:pairs, 0:1] * acc_all[0].astype(F32)
+    for j in range(1, n):
+        total = total + weight[:pairs, j:j + 1] * acc_all[j].astype(F32)
     for b in range(batch):
-        acc_out[plane, b * group:(b + 1) * group] = sums[b]
-    acc_out[plane, batch * group:] = jnp.where(stat_lane < batch, top, pltpu.roll(count, batch, 1))
-    sends += gather_start(acc_out, plane, outer, sd, rd, outer_peer)
-    gather_wait(acc_out, plane, outer, sd, rd, outer_peer)
-    top, count, sums = merge(acc_out, outer)
-    for b in range(batch):
-        att_rows[b] = sums[b] / count[:, b:b + 1]
+        att_rows[b] = total[b * group:(b + 1) * group]
     attended = jnp.concatenate([att_rows[:, h, :].astype(BF16) for h in range(group)], -1)
 
     loads[5].wait()
@@ -192,7 +185,7 @@
     total = kv_buf[0]
     for j in range(1, kv_size):
         total = total + kv_buf[j]
-    out[...] = total.astype(BF16)
+    out[...] = total
     for cp in sends:
         cp.wait_send()
 
@@ -210,13 +203,12 @@
     half = np.float64(ROPE_THETA) ** (-np.arange(0, head, 2, dtype=np.float64) / head)
     freq = jnp.asarray(np.concatenate([half, half]).astype(np.float32)[None, :])
     dma = pltpu.SemaphoreType.DMA
-    acc_rows = batch * group + group
     smem = pl.BlockSpec(memory_space=pltpu.SMEM)
     vmem = pl.BlockSpec(memory_space=pltpu.VMEM)
     hbm = pl.BlockSpec(memory_space=pl.ANY)
     return pl.pallas_call(
-        functools.partial(kernel, inner, outer, kv_size, group, head),
-        out_shape=jax.ShapeDtypeStruct((batch, cols), BF16),
+        functools.partial(kernel, n, inner, outer, kv_size, group, head),
+        out_shape=pltpu.VMEM((batch, cols), F32),
         in_specs=[smem, smem, vmem] + [hbm] * 6,
         out_specs=vmem,
         scratch_shapes=[
@@ -228,20 +220,20 @@
             pltpu.VMEM(vals.shape, BF16),
             pltpu.VMEM((inner, batch, qw + wkv.shape[1]), F32),
             pltpu.VMEM((outer, batch, qw + wkv.shape[1]), F32),
-            pltpu.VMEM((inner, acc_rows, head), F32),
-            pltpu.VMEM((outer, acc_rows, head), F32),
+            pltpu.VMEM((n, batch * group, head), BF16),
+            pltpu.VMEM((n, 1, head), F32),
             pltpu.VMEM((kv_size, batch, cols), F32),
             pltpu.VMEM((batch, group, head), F32),
             pltpu.VMEM((batch, group, head), F32),
             dma((6,)),
             dma((inner,)), dma((inner,)),
             dma((outer,)), dma((outer,)),
-            dma((inner,)), dma((inner,)),
-            dma((outer,)), dma((outer,)),
+            dma((n,)), dma((n,)),
+            dma((n,)), dma((n,)),
             dma((kv_size,)), dma((kv_size,)),
         ],
         compiler_params=pltpu.CompilerParams(collective_id=0, has_side_effects=True),
-    )(live, owner, freq, x, wq, wkv, wo, keys, vals)
+    )(live, owner, freq, x, wq, wkv, wo, keys, vals).astype(BF16)
 
 
 def solution(mesh):

time: 26.3 us -> 22.7 us (0.86)
  Pallas kernels: 24.8 us -> 21.9 us
  local copies, waits for them, and re-layouts: 1.28 us -> 0 us
  other arithmetic: 0 us -> 0.6 us
    pallas_call x1, Pallas kernels: 24.8 us -> 21.9 us  [local(): pl.pallas_call(functools.partial(kernel, n, inner, outer, kv_size, group,...]
    unnamed x1 -> x0, local copies, waits for them, and re-layouts: 1.28 us -> none
    convert_element_type x0 -> x1, other arithmetic: none -> 0.6 us  [local(): return pl.pallas_call(functools.partial(kernel, n, inner, outer, kv_size,...]
where the time goes in v3:
time: 22.7 us; the launch traced here: 22.5 us
  Pallas kernels  21.9 us (96%)
  other arithmetic  0.6 us (3%)
    pallas_call x1, Pallas kernels, local(): pl.pallas_call(functools.partial(kernel, n, inner, outer, kv_size, group,...  21.9 us
    convert_element_type x1, other arithmetic, local(): return pl.pallas_call(functools.partial(kernel, n, inner, outer, kv_size,...  0.6 us

profile of v3, /device:TPU:0, one launch (start us, length us, event | category | flops | bytes accessed | tf_op | source)
XLA Modules:
  0.0 22.5 jit_solution(18176103943442591729)
XLA Ops:
  0.0 21.9 %shard_map.91 = f32[4,512]{1,0:T(4,128)S(1)} custom-call(s32[4,16]{1,0:T(4,128)} %live.1, s32[4]{0:T(128)} %owner.1, f32[1,128]{1,0:T(1,128)} %constant.2.clone.freq, bf16[4,8192]{1,0:T(4,128)(2,1)} %x_hbm.1, bf16[512,1024]{1,0:T(8,128)(2,1)} %wq_hbm.1, bf16[512,256]{1,0:T(8,128)(2,1)} %wkv_hbm.1, bf16[1024,512]{1,0:T(8,128)(2,1)} %wo_hbm.1, ...), custom_call_target="tpu_custom_call" | custom-call | tf_op jit(solution)/shard_map/pallas_call | solution.py:209
  21.9 0.6 %convert_element_type.3 = bf16[4,512]{1,0:T(4,128)(2,1)} convert(f32[4,512]{1,0:T(4,128)S(1)} %shard_map.91) | non-fusion elementwise | flops 2048 | bytes 12288 | tf_op jit(solution)/shard_map/convert_element_type | solution.py:236

commit v4 on v3

--- a/solution.py
+++ b/solution.py
@@ -50,7 +50,7 @@
     out,
     x, wq, wkv, wo, keys, vals,
     part_in, part_out, acc_all, stat_all, kv_buf, q_rows, att_rows,
-    load_sem, sa, ra, sb, rb, sc, rc, sd, rd, se, re,
+    load_sem, sa, ra, sb, rb, sc, rc, sd, rd, se, re, relay_sem,
 ):
     me = lax.axis_index("seq")
     kv = lax.axis_index("kv")
@@ -77,8 +77,13 @@
     for d in range(1, inner):
         pl.semaphore_signal(barrier, inc=1, device_id=inner_peer(lax.rem(spot + d, inner)),
                             device_id_type=pl.DeviceIdType.MESH)
-    for d in range(1, outer):
-        pl.semaphore_signal(barrier, inc=1, device_id=outer_peer(lax.rem(plane + d, outer)),
+    steps = [1 << i for i in range(outer.bit_length() - 1)]
+
+    def across(step):
+        return outer_peer(plane + step - 2 * step * lax.rem(plane // step, 2))
+
+    for step in steps:
+        pl.semaphore_signal(barrier, inc=1, device_id=across(step),
                             device_id_type=pl.DeviceIdType.MESH)
     for d in range(1, kv_size):
         pl.semaphore_signal(barrier, inc=1, device_id=kv_peer(lax.rem(kv + d, kv_size)),
@@ -117,9 +122,14 @@
     xs = x[...]
     part_in[spot, :, :qw] = jnp.dot(xs, wq[...], preferred_element_type=F32)
     part_in[spot, :, qw:] = jnp.dot(xs, wkv[...], preferred_element_type=F32)
-    pl.semaphore_wait(barrier, inner + outer + kv_size - 3)
+    pl.semaphore_wait(barrier, inner - 1 + len(steps) + kv_size - 1)
 
     sends = gather_start(part_in, spot, inner, sa, ra, inner_peer)
+    for i in range(len(steps) - 1):
+        for step in steps:
+            pl.semaphore_signal(relay_sem.at[i], inc=1, device_id=across(step),
+                                device_id_type=pl.DeviceIdType.MESH)
+        pl.semaphore_wait(relay_sem.at[i], len(steps))
     gather_wait(part_in, spot, inner, sa, ra, inner_peer)
     total = part_in[0]
     for j in range(1, inner):
@@ -231,6 +241,7 @@
             dma((n,)), dma((n,)),
             dma((n,)), dma((n,)),
             dma((kv_size,)), dma((kv_size,)),
+            pltpu.SemaphoreType.REGULAR((max(outer.bit_length() - 2, 1),)),
         ],
         compiler_params=pltpu.CompilerParams(collective_id=0, has_side_effects=True),
     )(live, owner, freq, x, wq, wkv, wo, keys, vals).astype(BF16)

time: 22.7 us -> 22.1 us (0.974)
  Pallas kernels: 21.9 us -> 21.3 us
    pallas_call x1, Pallas kernels: 21.9 us -> 21.3 us  [local(): pl.pallas_call(functools.partial(kernel, n, inner, outer, kv_size, group,...]
where the time goes in v4:
time: 22.1 us; the launch traced here: 21.9 us
  Pallas kernels  21.3 us (96%)
  other arithmetic  0.6 us (3%)
    pallas_call x1, Pallas kernels, local(): pl.pallas_call(functools.partial(kernel, n, inner, outer, kv_size, group,...  21.3 us
    convert_element_type x1, other arithmetic, local(): return pl.pallas_call(functools.partial(kernel, n, inner, outer, kv_size,...  0.6 us

profile of v4, /device:TPU:0, one launch (start us, length us, event | category | flops | bytes accessed | tf_op | source)
XLA Modules:
  0.0 21.9 jit_solution(16805728927854783607)
XLA Ops:
  0.0 21.3 %shard_map.91 = f32[4,512]{1,0:T(4,128)S(1)} custom-call(s32[4,16]{1,0:T(4,128)} %live.1, s32[4]{0:T(128)} %owner.1, f32[1,128]{1,0:T(1,128)} %constant.2.clone.freq, bf16[4,8192]{1,0:T(4,128)(2,1)} %x_hbm.1, bf16[512,1024]{1,0:T(8,128)(2,1)} %wq_hbm.1, bf16[512,256]{1,0:T(8,128)(2,1)} %wkv_hbm.1, bf16[1024,512]{1,0:T(8,128)(2,1)} %wo_hbm.1, ...), custom_call_target="tpu_custom_call" | custom-call | tf_op jit(solution)/shard_map/pallas_call | solution.py:219
  21.3 0.6 %convert_element_type.3 = bf16[4,512]{1,0:T(4,128)(2,1)} convert(f32[4,512]{1,0:T(4,128)S(1)} %shard_map.91) | non-fusion elementwise | flops 2048 | bytes 12288 | tf_op jit(solution)/shard_map/convert_element_type | solution.py:247
